TPU v7x, 32 devices: a whole 2x2x4 slice. The times are simulated.
32 devices in a mesh: dp: 8 (over y, x, core), seq: 4 (over z).
Axes of the slice: x: 2, y: 2, z: 4, core: 2. Of those that a mesh axis runs over, the one named last changes fastest.
Arguments:
- tile_tokens: bfloat16 [8, 128, 3200], P('dp', 'seq'), may hold values from -6 to 6
- proj_weight: bfloat16 [3200, 8192], P('dp', 'seq')
- text_hidden: bfloat16 [8, 512, 8192], P('dp', 'seq'), may hold values from -6 to 6
- cotangent: bfloat16 [8, 512, 8192], P('dp', 'seq'), may hold values from -1.1953125 to 1.1953125
- norm_gain: float32 [8192], replicated, may hold values from 0.25 to 1.75
- placeholders: int32 [8, 128], P('dp'), may hold values from 0 to 511, as said below
- bucket_levels: int32 [8, 4, 3200], P('dp', 'seq'), may hold values from 2 to 16
- row_draws: float32 [8, 4, 3200], P('dp', 'seq'), may hold values from 0 to 1
- column_draws: float32 [8, 8192], P('dp', 'seq'), may hold values from 0 to 1
Outputs:
- weight_grad: float32 [3200, 8192], P('dp', 'seq')
- gain_grad: float32 [8192], replicated
Inputs may be any that keep to these rules, and one draw needn't show every extreme that they name: Each row is strictly increasing. Among the positions of one device's block of 128 positions stand at most 48 placeholders, and in every row some block holds exactly 48.
All inputs are finite; a program needn't handle non-finite values.
Results may differ from a plain program's by a relative error of at most 0.014.
Values may be sent and summed in bfloat16 or wider, within the bound.
No kernel may reach another device: no remote copies, remote signals or barrier semaphores. Data moves between devices by JAX's collectives and lax.ppermute only.
A program may use at most 64 MiB of HBM per device.

v0:
```python
import jax
import jax.numpy as jnp
from jax import lax
from jax.sharding import PartitionSpec as P

IMG_MOST = 48
EPSILON = 1e-06


def quantize(gradient, levels_now, rows_now, columns_now):
    bucket_norm = jnp.sqrt(jnp.sum(gradient * gradient, axis=1, keepdims=True) + EPSILON)
    step_count = levels_now.astype(jnp.float32)[:, None]
    offset = 0.25 + 0.25 * (rows_now[:, None] + columns_now[None, :])
    ratio = jnp.abs(gradient) / bucket_norm * step_count
    lower = jnp.floor(ratio)
    quantum = lower + jnp.clip(2.0 * (ratio - lower - offset) + 0.5, 0.0, 1.0)
    return jnp.sign(gradient) * bucket_norm * quantum / step_count


def on_device(
    tile_tokens,
    proj_weight,
    text_hidden,
    cotangent,
    norm_gain,
    placeholders,
    bucket_levels,
    row_draws,
    column_draws,
):
    seq_count = lax.axis_size("seq")
    seq_index = lax.axis_index("seq")
    replicas = lax.axis_size("dp")
    places = placeholders[0]
    image_total = places.shape[0]
    tok_rows = text_hidden.shape[1]
    model_width = text_hidden.shape[2]
    columns = proj_weight.shape[1]
    all_positions = tok_rows * seq_count
    zero_half = jnp.zeros((), jnp.bfloat16)
    own_text = text_hidden[0]
    own_cot = cotangent[0]
    gathered = lax.all_gather(tile_tokens[0], "seq", axis=0, tiled=True)
    patch_block = gathered
    embedded = jnp.dot(
        patch_block,
        lax.all_gather(proj_weight, "dp", axis=0, tiled=True),
        preferred_element_type=jnp.float32,
    ).astype(jnp.bfloat16)
    image_marks = jnp.zeros((all_positions,), jnp.int32).at[places].set(1)
    local_marks = lax.dynamic_slice_in_dim(image_marks, seq_index * tok_rows, tok_rows)
    is_image = local_marks[:, None] == 1
    owners = places // tok_rows
    owner_ids = jnp.arange(seq_count, dtype=jnp.int32)
    counts = jnp.sum((owners[:, None] == owner_ids[None, :]).astype(jnp.int32), axis=0)
    starts = jnp.cumsum(counts) - counts
    own_start = starts[seq_index]
    own_count = counts[seq_index]
    slot_ids = jnp.arange(IMG_MOST, dtype=jnp.int32)
    source_rows = jnp.clip(own_start + slot_ids, 0, image_total - 1)
    local_slots = jnp.clip(jnp.take(places, source_rows) - seq_index * tok_rows, 0, tok_rows - 1)
    slot_live = (slot_ids < own_count)[:, None]
    flat_index = owners * IMG_MOST + (
        jnp.arange(image_total, dtype=jnp.int32) - jnp.take(starts, owners)
    )
    outgoing = jnp.where(slot_live, jnp.take(own_cot, local_slots, axis=0), zero_half)
    returned = lax.all_to_all(outgoing[None], "seq", split_axis=2, concat_axis=0, tiled=True)
    image_cot = jnp.take(returned.reshape(-1, columns), flat_index, axis=0).astype(jnp.float32)
    emb_float = embedded.astype(jnp.float32)
    column_gain = lax.dynamic_slice_in_dim(norm_gain, seq_index * columns, columns)
    grad_in = image_cot * column_gain[None, :]
    squares, mixed = lax.psum(
        (jnp.sum(emb_float * emb_float, axis=1), jnp.sum(grad_in * emb_float, axis=1)), "seq"
    )
    inverse = lax.rsqrt(squares / model_width + EPSILON)[:, None]
    normed = emb_float * inverse
    emb_grad = ((grad_in - normed * (mixed[:, None] * inverse / model_width)) * inverse).astype(
        jnp.bfloat16
    )
    image_part = jnp.sum(image_cot * normed, axis=0)
    text_float = own_text.astype(jnp.float32)
    text_inverse = lax.rsqrt(jnp.mean(text_float * text_float, axis=1, keepdims=True) + EPSILON)
    text_terms = own_cot.astype(jnp.float32) * text_float * text_inverse
    text_part = jnp.sum(jnp.where(is_image, 0.0, text_terms), axis=0)
    placed_part = lax.dynamic_update_slice_in_dim(
        jnp.zeros((model_width,), jnp.float32), image_part, seq_index * columns, 0
    )
    gain_part = text_part + placed_part
    own_levels = bucket_levels[0, 0]
    own_row_draws = row_draws[0, 0]
    own_column_draws = column_draws[0]
    patch_block = gathered
    gradient = lax.dot_general(
        patch_block, emb_grad, (((0,), (0,)), ((), ())), preferred_element_type=jnp.float32
    )
    summed = lax.psum_scatter(
        quantize(gradient, own_levels, own_row_draws, own_column_draws).astype(jnp.bfloat16),
        "dp",
        scatter_dimension=0,
        tiled=True,
    ).astype(jnp.float32)
    gain_total = lax.psum(gain_part, ("dp", "seq"))
    return (summed / replicas, gain_total / replicas)


def solution(mesh):
    return jax.shard_map(
        on_device,
        mesh=mesh,
        in_specs=(
            P("dp", "seq", None),
            P("dp", "seq"),
            P("dp", "seq", None),
            P("dp", "seq", None),
            P(),
            P("dp", None),
            P("dp", "seq", None),
            P("dp", "seq", None),
            P("dp", "seq"),
        ),
        out_specs=(P("dp", "seq"), P()),
        check_vma=False,
    )
```

profile of v0, /device:TPU:0, one launch (start us, length us, event | category | flops | bytes accessed | tf_op | source)
XLA Modules:
  0.0 315.0 jit_solution(2458585537406789046)
XLA Ops:
  10.9 1.4 gather_fusion
  13.0 3.6 %gather_fusion.1 = bf16[48,8192]{1,0:T(8,128)(2,1)S(1)} fusion(bf16[128,8192]{1,0:T(8,128)(2,1)} %bitcast.74, s32[1024]{0:T(1024)S(1)} %pad_clamp_fusion.1), kind=kCustom, calls=%fused_computation.1 | custom fusion | bytes 1573056 | tf_op jit(solution)/shard_map/jit(_take)/gather | solution.py:66
  16.6 1.3 compare_and_fusion
  18.1 6.8 %copy.22 = bf16[1,48,8192]{1,0,2:T(2,128)(2,1)} copy(bf16[1,48,8192]{2,1,0:T(8,128)(2,1)S(1)} %fusion.21) | data formatting | bytes 1572864 | tf_op jit(solution)/shard_map/jit(_where)/select_n | solution.py:66
  25.3 45.2 %reduce.4 = bf16[8192,48]{1,0:T(8,128)(2,1)S(1)} reduce(bf16[8192,1,48]{2,1,0:T(2,128)(2,1)} %bitcast.76, bf16[]{:T(256)} %broadcast.575), dimensions={1}, to_apply=%bitcast.63.reduce_sub_computation | reduce | bytes 1572866
  70.6 4.0 %reshape.423 = bf16[4,2,49152]{2,1,0:T(2,128)(2,1)} reshape(bf16[8192,48]{1,0:T(8,128)(2,1)S(1)} %reduce.4) | data formatting | bytes 1572864
  74.6 6.3 %all-to-all-start = ((bf16[4,2,49152]{2,1,0:T(2,128)(2,1)}), bf16[4,2,49152]{2,1,0:T(2,128)(2,1)S(1)}, u32[]{:S(2)}, u32[]{:S(2)}) async-start(bf16[4,2,49152]{2,1,0:T(2,128)(2,1)} %reshape.423), calls=%async_computation | async-start | bytes 1572864 | tf_op jit(solution)/shard_map/all_to_all | solution.py:67
  81.7 2.6 compare_and_fusion.1
  84.4 30.7 %all-gather = bf16[1,128,3200]{2,1,0:T(8,128)(2,1)S(1)} all-gather(bf16[1,32,3200]{2,1,0:T(8,128)(2,1)S(1)} %copy-done.4), channel_id=2, replica_groups=mesh['dp'=8,'seq'=4] {'seq'}, dimensions={1}, use_global_device_ids=true | all-gather | bytes 1024000 | tf_op jit(solution)/shard_map/all_gather | solution.py:43
  115.0 4.6 %reshape.424 = bf16[8192,1,48]{2,1,0:T(2,128)(2,1)} reshape(bf16[4,2,49152]{2,1,0:T(2,128)(2,1)S(1)} %all-to-all-done) | data formatting | bytes 1572864
  119.6 8.1 %copy.23 = bf16[1,48,8192]{2,1,0:T(8,128)(2,1)S(1)} copy(bf16[1,48,8192]{1,0,2:T(2,128)(2,1)} %bitcast.77) | data formatting | bytes 1572864 | tf_op jit(solution)/shard_map/all_to_all | solution.py:67
  129.8 7.1 %multiply_reduce_fusion.1 = (f32[128]{0:T(128)S(1)}, f32[128,2048]{1,0:T(8,128)S(1)}) fusion(bf16[3200,2048]{1,0:T(8,128)(2,1)} %all-gather.3.cloned.1.call-done, bf16[1,128,3200]{2,1,0:T(8,128)(2,1)S(1)} %all-gather), kind=kOutput, calls=%fused_computation.31 | convolution fusion | flops 1678770048 | bytes 14975488 | tf_op jit(solution)/shard_map/dot_general | solution.py:45
  136.9 11.1 %psum.21 = f32[128]{0:T(128)S(1)} all-reduce(f32[128]{0:T(128)S(1)} %get-tuple-element.22), channel_id=1, replica_groups=mesh['dp'=8,'seq'=4] {'seq'}, use_global_device_ids=true, to_apply=%region_3.4 | all-reduce | flops 128 | bytes 1024 | tf_op jit(solution)/shard_map/psum | solution.py:72
  148.4 8.4 %psum.22 = f32[128]{0:T(128)S(1)} all-reduce(f32[128]{0:T(128)S(1)} %get-tuple-element.13), channel_id=1, replica_groups=mesh['dp'=8,'seq'=4] {'seq'}, use_global_device_ids=true, to_apply=%region_5.6 | all-reduce | flops 128 | bytes 1024 | tf_op jit(solution)/shard_map/psum | solution.py:72
  156.8 5.1 %multiply_reduce_fusion = (f32[3200]{0:T(1024)S(1)}, f32[2048,3200]{1,0:T(8,128)S(1)}) fusion(bf16[1,128,3200]{2,1,0:T(8,128)(2,1)S(1)} %all-gather, f32[128,2048]{1,0:T(8,128)} %copy-done.2, f32[128]{0:T(128)S(1)} %multiply_multiply_fusion, f32[128]{0:T(128)S(1)} %add_rsqrt_fusion.1, f32[2048]{0:T(1024)S(1)} %dynamic_slice.14, ...), kind=kOutput, calls=%fused_computation.12 | convolution fusion | flops 1692922752 | bytes 28628608 | tf_op jit(solution)/shard_map/dot_general | solution.py:93
  162.0 22.2 %fusion.6 = bf16[3200,2048]{0,1:T(8,128)(2,1)} fusion(f32[2048,3200]{1,0:T(8,128)S(1)} %get-tuple-element.25, f32[3200]{0:T(1024)S(1)} %convert_reduce_fusion, f32[2048]{0:T(1024)S(1)} %bitcast.79, f32[3200]{0:T(1024)S(1)} %reduce.2, f32[3200]{0:T(1024)S(1)} %add_sqrt_fusion), kind=kLoop, calls=%fused_computation.13 | loop fusion | flops 117964800 | bytes 39368192 | tf_op jit(solution)/shard_map/convert_element_type | solution.py:97
  184.1 18.3 %copy.26 = bf16[3200,2048]{1,0:T(8,128)(2,1)} copy(bf16[3200,2048]{0,1:T(8,128)(2,1)} %fusion.6) | data formatting | bytes 26214400
  203.6 2.1 fusion.10
  205.7 2.6 fusion.9
  208.3 41.3 %psum.23 = f32[8192]{0:T(1024)S(1)} all-reduce(f32[8192]{0:T(1024)S(1)} %add_dynamic-update-slice_fusion), channel_id=1, replica_groups=mesh['dp'=8,'seq'=4] {'dp','seq'}, use_global_device_ids=true, to_apply=%region_12.13 | all-reduce | flops 8192 | bytes 65536 | tf_op jit(solution)/shard_map/psum | solution.py:102
  250.3 47.4 %reduce-scatter.4.cloned.1.call-done = bf16[400,2048]{1,0:T(8,128)(2,1)} async-done(((bf16[3200,2048]{1,0:T(8,128)(2,1)}), bf16[400,2048]{1,0:T(8,128)(2,1)}) %reduce-scatter.4.cloned.1.call-update) | async-done | bytes 1638416
  297.7 2.8 copy.27
  300.5 2.5 convert_multiply_fusion.2
  303.0 5.2 %copy.25 = f32[400,2048]{1,0:T(8,128)} copy(f32[400,2048]{0,1:T(8,128)} %convert_multiply_fusion.2) | data formatting | bytes 6553600
  (53 shorter events, 10.0 us)
Async XLA Ops:
  7.2 74.5 %copy-start = (s32[1,128]{1,0:T(1,128)S(1)}, s32[1,128]{1,0:T(1,128)}, u32[]{:S(2)}) copy-start(s32[1,128]{1,0:T(1,128)} %param.14) | copy-start | bytes 1540
  7.2 74.5 %copy-start.6 = (f32[1,1,3200]{2,1,0:T(1,128)S(1)}, f32[1,1,3200]{2,1,0:T(1,128)}, u32[]{:S(2)}) copy-start(f32[1,1,3200]{2,1,0:T(1,128)} %param.16) | copy-start | bytes 38404
  7.2 77.1 %copy-start.5 = (s32[1,1,3200]{2,1,0:T(1,128)S(1)}, s32[1,1,3200]{2,1,0:T(1,128)}, u32[]{:S(2)}) copy-start(s32[1,1,3200]{2,1,0:T(1,128)} %param.15) | copy-start | bytes 38404
  7.2 77.2 %copy-start.4 = (bf16[1,32,3200]{2,1,0:T(8,128)(2,1)S(1)}, bf16[1,32,3200]{2,1,0:T(8,128)(2,1)}, u32[]{:S(2)}) copy-start(bf16[1,32,3200]{2,1,0:T(8,128)(2,1)} %param.9) | copy-start | bytes 614404
  7.2 122.6 %all-gather.3.cloned.1.call-start = ((), (), s32[]{:S(2)}) async-start(), calls=%async_computation.2 | async-start | bytes 14745600 | tf_op jit(solution)/shard_map/all_gather | solution.py:47
  74.6 40.5 %all-to-all-start = ((bf16[4,2,49152]{2,1,0:T(2,128)(2,1)}), bf16[4,2,49152]{2,1,0:T(2,128)(2,1)S(1)}, u32[]{:S(2)}, u32[]{:S(2)}) async-start(bf16[4,2,49152]{2,1,0:T(2,128)(2,1)} %reshape.423), calls=%async_computation | async-start | bytes 1572864 | tf_op jit(solution)/shard_map/all_to_all | solution.py:67
  80.9 216.8 %reduce-scatter.4.cloned.1.call-start = ((), (), s32[]{:S(2)}) async-start(), calls=%async_computation.3 | async-start | bytes 14745600
  129.7 27.0 %copy-start.3 = (bf16[128,2048]{1,0:T(8,128)(2,1)}, bf16[128,2048]{1,0:T(8,128)(2,1)S(1)}, u32[]{:S(2)}) copy-start(bf16[128,2048]{1,0:T(8,128)(2,1)S(1)} %gather_fusion.2) | copy-start | bytes 1572868
  136.8 19.9 %copy-start.2 = (f32[128,2048]{1,0:T(8,128)}, f32[128,2048]{1,0:T(8,128)S(1)}, u32[]{:S(2)}) copy-start(f32[128,2048]{1,0:T(8,128)S(1)} %get-tuple-element.23) | copy-start | bytes 3145732
  156.8 5.2 %copy-start.7 = (f32[1,2048]{1,0:T(1,128)S(1)}, f32[1,2048]{1,0:T(1,128)}, u32[]{:S(2)}) copy-start(f32[1,2048]{1,0:T(1,128)} %param.17) | copy-start | bytes 24580
  202.5 3.2 %copy-start.1 = (bf16[1,128,8192]{2,1,0:T(8,128)(2,1)S(1)}, bf16[1,128,8192]{2,1,0:T(8,128)(2,1)}, u32[]{:S(2)}) copy-start(bf16[1,128,8192]{2,1,0:T(8,128)(2,1)} %param.12) | copy-start | bytes 6291460
Sparse Core Ops, SparseCore 0:
  9.9 76.9 all-gather.2
  202.6 95.0 reduce-scatter.3
where the time goes:
time: 316 us; the launch traced here: 315 us
  blocking collectives  91.5 us (29%)
  other arithmetic  82.2 us (26%)
  local copies, waits for them, and re-layouts  60.3 us (19%)
  waiting for transfers between devices  48.1 us (15%)
  between operations  14.3 us (5%)
  matrix products  12.2 us (4%)
  starting transfers between devices  6.39 us (2%)
    unnamed x3, waiting for transfers between devices  48.1 us
    unnamed x2, other arithmetic  45.3 us
    psum x1, blocking collectives, on_device(): gain_total = lax.psum(gain_part, ('dp', 'seq'))  41.3 us
    unnamed x22, local copies, waits for them, and re-layouts  35.4 us
    all_gather x1, blocking collectives, on_device(): gathered = lax.all_gather(tile_tokens[0], 'seq', axis=0, tiled=True)  30.7 us
    convert_element_type x1, other arithmetic, on_device(): quantize(gradient, own_levels, own_row_draws, own_column_draws)  22.2 us
    psum x2, blocking collectives, on_device(): lax.psum((jnp.sum(emb_float * emb_float, axis=1), jnp.sum(grad_in * emb_f...  19.5 us
    all_to_all x3, local copies, waits for them, and re-layouts, on_device(): lax.all_to_all(outgoing[None], 'seq', split_axis=2, concat_axis=0, tiled=...  9.14 us
  transfers between devices with their start and end apart: 3, of which 1 were waited for; matrix products, arithmetic and copies ran while one was open for 29% of the time, Pallas kernels for 0%

commit v1 on v0

--- a/solution.py
+++ b/solution.py
@@ -99,7 +99,7 @@
         scatter_dimension=0,
         tiled=True,
     ).astype(jnp.float32)
-    gain_total = lax.psum(gain_part, ("dp", "seq"))
+    gain_total = jnp.sum(lax.all_gather(gain_part, ("dp", "seq")), axis=0)
     return (summed / replicas, gain_total / replicas)
 
 

time: 316 us -> 347 us (1.098)
  waiting for transfers between devices: 48.1 us -> 106 us
  blocking collectives: 91.5 us -> 47 us
  other arithmetic: 82.2 us -> 87.9 us
  matrix products: 12.2 us -> 17.6 us
  local copies, waits for them, and re-layouts: 60.3 us -> 65.5 us
    unnamed x3 -> x4, waiting for transfers between devices: 48.1 us -> 95.5 us
    psum x1 -> x0, blocking collectives: 41.3 us -> none  [on_device(): gain_total = lax.psum(gain_part, ('dp', 'seq'))]
    all_gather x0 -> x1, waiting for transfers between devices: none -> 10.8 us  [on_device(): gain_total = jnp.sum(lax.all_gather(gain_part, ('dp', 'seq')), axis=0)]
    dot_general x1, matrix products: 5.14 us -> 10.7 us  [on_device(): lax.dot_general(patch_block, emb_grad, (((0,), (0,)), ((), ())), preferre...]
    unnamed x22 -> x20, local copies, waits for them, and re-layouts: 35.4 us -> 38.3 us
  transfers between devices with their start and end apart: 3 -> 4, of which waited for: 1 -> 2; matrix products, arithmetic and copies ran while one was open for 29% -> 41% of each run, Pallas kernels for 0% -> 0%
where the time goes in v1:
time: 347 us; the launch traced here: 345 us
  waiting for transfers between devices  106 us (31%)
  other arithmetic  87.9 us (25%)
  local copies, waits for them, and re-layouts  65.5 us (19%)
  blocking collectives  47 us (14%)
  matrix products  17.6 us (5%)
  between operations  14 us (4%)
  starting transfers between devices  6.75 us (2%)
    unnamed x4, waiting for transfers between devices  95.5 us
    unnamed x2, other arithmetic  46.5 us
    unnamed x20, local copies, waits for them, and re-layouts  38.3 us
    all_gather x1, blocking collectives, on_device(): gathered = lax.all_gather(tile_tokens[0], 'seq', axis=0, tiled=True)  27.5 us
    convert_element_type x1, other arithmetic, on_device(): quantize(gradient, own_levels, own_row_draws, own_column_draws)  24.2 us
    psum x2, blocking collectives, on_device(): lax.psum((jnp.sum(emb_float * emb_float, axis=1), jnp.sum(grad_in * emb_f...  19.5 us
    all_gather x1, waiting for transfers between devices, on_device(): gain_total = jnp.sum(lax.all_gather(gain_part, ('dp', 'seq')), axis=0)  10.8 us
    dot_general x1, matrix products, on_device(): lax.dot_general(patch_block, emb_grad, (((0,), (0,)), ((), ())), preferre...  10.7 us
  transfers between devices with their start and end apart: 4, of which 2 were waited for; matrix products, arithmetic and copies ran while one was open for 41% of the time, Pallas kernels for 0%

profile of v1, /device:TPU:0, one launch (start us, length us, event | category | flops | bytes accessed | tf_op | source)
XLA Modules:
  0.0 345.0 jit_solution(14568055128248389789)
XLA Ops:
  10.8 1.4 gather_fusion
  13.0 3.8 %gather_fusion.1 = bf16[48,8192]{1,0:T(8,128)(2,1)S(1)} fusion(bf16[128,8192]{1,0:T(8,128)(2,1)} %bitcast.76, s32[1024]{0:T(1024)S(1)} %pad_clamp_fusion.1), kind=kCustom, calls=%fused_computation.1 | custom fusion | bytes 1573056 | tf_op jit(solution)/shard_map/jit(_take)/gather | solution.py:66
  19.1 8.9 %copy.22 = bf16[1,48,8192]{1,0,2:T(2,128)(2,1)} copy(bf16[1,48,8192]{2,1,0:T(8,128)(2,1)} %fusion.21) | data formatting | bytes 1572864 | tf_op jit(solution)/shard_map/jit(_where)/select_n | solution.py:66
  28.5 46.5 %reduce.5 = bf16[8192,48]{1,0:T(8,128)(2,1)} reduce(bf16[8192,1,48]{2,1,0:T(2,128)(2,1)} %bitcast.78, bf16[]{:T(256)} %broadcast.575), dimensions={1}, to_apply=%bitcast.65.reduce_sub_computation | reduce | bytes 1572866
  74.9 5.1 %reshape.431 = bf16[4,2,49152]{2,1,0:T(2,128)(2,1)} reshape(bf16[8192,48]{1,0:T(8,128)(2,1)} %reduce.5) | data formatting | bytes 1572864
  80.0 6.5 %all-to-all-start = ((bf16[4,2,49152]{2,1,0:T(2,128)(2,1)}), bf16[4,2,49152]{2,1,0:T(2,128)(2,1)}, u32[]{:S(2)}, u32[]{:S(2)}) async-start(bf16[4,2,49152]{2,1,0:T(2,128)(2,1)} %reshape.431), calls=%async_computation | async-start | bytes 1572864 | tf_op jit(solution)/shard_map/all_to_all | solution.py:67
  87.5 2.5 compare_and_fusion.1
  90.9 2.1 fusion.10
  93.0 27.5 %all-gather = bf16[1,128,3200]{2,1,0:T(8,128)(2,1)S(1)} all-gather(bf16[1,32,3200]{2,1,0:T(8,128)(2,1)S(1)} %copy-done.2), channel_id=2, replica_groups=mesh['dp'=8,'seq'=4] {'seq'}, dimensions={1}, use_global_device_ids=true | all-gather | bytes 1024000 | tf_op jit(solution)/shard_map/all_gather | solution.py:43
  120.5 2.5 fusion.9
  123.0 5.8 %reshape.432 = bf16[8192,1,48]{2,1,0:T(2,128)(2,1)} reshape(bf16[4,2,49152]{2,1,0:T(2,128)(2,1)} %all-to-all-done) | data formatting | bytes 1572864
  128.8 8.1 %copy.23 = bf16[1,48,8192]{2,1,0:T(8,128)(2,1)S(1)} copy(bf16[1,48,8192]{1,0,2:T(2,128)(2,1)} %bitcast.79) | data formatting | bytes 1572864 | tf_op jit(solution)/shard_map/all_to_all | solution.py:67
  138.9 6.9 %multiply_reduce_fusion.1 = (f32[128]{0:T(128)S(1)}, f32[128,2048]{1,0:T(8,128)S(1)}) fusion(bf16[3200,2048]{1,0:T(8,128)(2,1)} %all-gather.5.cloned.1.call-done, bf16[1,128,3200]{2,1,0:T(8,128)(2,1)S(1)} %all-gather), kind=kOutput, calls=%fused_computation.31 | convolution fusion | flops 1678770048 | bytes 14975488 | tf_op jit(solution)/shard_map/dot_general | solution.py:45
  145.8 11.1 %psum.14 = f32[128]{0:T(128)S(1)} all-reduce(f32[128]{0:T(128)S(1)} %get-tuple-element.22), channel_id=1, replica_groups=mesh['dp'=8,'seq'=4] {'seq'}, use_global_device_ids=true, to_apply=%region_3.4 | all-reduce | flops 128 | bytes 1024 | tf_op jit(solution)/shard_map/psum | solution.py:72
  157.3 8.4 %psum.15 = f32[128]{0:T(128)S(1)} all-reduce(f32[128]{0:T(128)S(1)} %get-tuple-element.13), channel_id=1, replica_groups=mesh['dp'=8,'seq'=4] {'seq'}, use_global_device_ids=true, to_apply=%region_5.6 | all-reduce | flops 128 | bytes 1024 | tf_op jit(solution)/shard_map/psum | solution.py:72
  165.7 10.7 %multiply_reduce_fusion = (f32[3200]{0:T(1024)S(1)}, f32[2048,3200]{1,0:T(8,128)}) fusion(bf16[1,128,3200]{2,1,0:T(8,128)(2,1)S(1)} %all-gather, f32[128,2048]{1,0:T(8,128)S(1)} %get-tuple-element.23, f32[128]{0:T(128)S(1)} %multiply_multiply_fusion, f32[128]{0:T(128)S(1)} %add_rsqrt_fusion.1, f32[2048]{0:T(1024)S(1)} %dynamic_slice.14, ...), kind=kOutput, calls=%fused_computation.12 | convolution fusion | flops 1692922752 | bytes 28628608 | tf_op jit(solution)/shard_map/dot_general | solution.py:93
  177.4 24.2 %fusion.6 = bf16[3200,2048]{0,1:T(8,128)(2,1)} fusion(f32[2048,3200]{1,0:T(8,128)} %get-tuple-element.25, f32[3200]{0:T(1024)S(1)} %convert_reduce_fusion, f32[2048]{0:T(1024)S(1)} %bitcast.83, f32[3200]{0:T(1024)S(1)} %reduce.3, f32[3200]{0:T(1024)S(1)} %add_sqrt_fusion), kind=kLoop, calls=%fused_computation.13 | loop fusion | flops 117964800 | bytes 39368192 | tf_op jit(solution)/shard_map/convert_element_type | solution.py:97
  201.5 18.3 %copy.26 = bf16[3200,2048]{1,0:T(8,128)(2,1)} copy(bf16[3200,2048]{0,1:T(8,128)(2,1)} %fusion.6) | data formatting | bytes 26214400
  219.9 10.8 %all-gather.7.cloned.1.call-done = f32[32,1,8192]{2,1,0:T(1,128)} async-done(((f32[1,1,8192]{2,1,0:T(1,128)}), f32[32,1,8192]{2,1,0:T(1,128)}) %all-gather.7.cloned.1.call-update) | async-done | bytes 1048592 | tf_op jit(solution)/shard_map/all_gather | solution.py:102
  230.7 1.9 reduce_sum.82
  233.2 94.8 %reduce-scatter.4.cloned.1.call-done = bf16[400,2048]{1,0:T(8,128)(2,1)} async-done(((bf16[3200,2048]{1,0:T(8,128)(2,1)}), bf16[400,2048]{1,0:T(8,128)(2,1)}) %reduce-scatter.4.cloned.1.call-update) | async-done | bytes 1638416
  328.0 2.8 copy.27
  330.8 2.5 convert_multiply_fusion.2
  333.3 5.2 %copy.25 = f32[400,2048]{1,0:T(8,128)} copy(f32[400,2048]{0,1:T(8,128)} %convert_multiply_fusion.2) | data formatting | bytes 6553600
  (55 shorter events, 13.0 us)
Async XLA Ops:
  7.2 79.3 %copy-start = (s32[1,128]{1,0:T(1,128)S(1)}, s32[1,128]{1,0:T(1,128)}, u32[]{:S(2)}) copy-start(s32[1,128]{1,0:T(1,128)} %param.14) | copy-start | bytes 1540
  7.2 82.8 %copy-start.4 = (s32[1,1,3200]{2,1,0:T(1,128)S(1)}, s32[1,1,3200]{2,1,0:T(1,128)}, u32[]{:S(2)}) copy-start(s32[1,1,3200]{2,1,0:T(1,128)} %param.15) | copy-start | bytes 38404
  7.2 83.6 %copy-start.5 = (f32[1,1,3200]{2,1,0:T(1,128)S(1)}, f32[1,1,3200]{2,1,0:T(1,128)}, u32[]{:S(2)}) copy-start(f32[1,1,3200]{2,1,0:T(1,128)} %param.16) | copy-start | bytes 38404
  7.2 131.7 %all-gather.5.cloned.1.call-start = ((), (), s32[]{:S(2)}) async-start(), calls=%async_computation.2 | async-start | bytes 14745600 | tf_op jit(solution)/shard_map/all_gather | solution.py:47
  13.0 80.0 %copy-start.2 = (bf16[1,32,3200]{2,1,0:T(8,128)(2,1)S(1)}, bf16[1,32,3200]{2,1,0:T(8,128)(2,1)}, u32[]{:S(2)}) copy-start(bf16[1,32,3200]{2,1,0:T(8,128)(2,1)} %param.9) | copy-start | bytes 614404
  13.0 107.5 %copy-start.1 = (bf16[1,128,8192]{2,1,0:T(8,128)(2,1)S(1)}, bf16[1,128,8192]{2,1,0:T(8,128)(2,1)}, u32[]{:S(2)}) copy-start(bf16[1,128,8192]{2,1,0:T(8,128)(2,1)} %param.12) | copy-start | bytes 6291460
  80.0 42.9 %all-to-all-start = ((bf16[4,2,49152]{2,1,0:T(2,128)(2,1)}), bf16[4,2,49152]{2,1,0:T(2,128)(2,1)}, u32[]{:S(2)}, u32[]{:S(2)}) async-start(bf16[4,2,49152]{2,1,0:T(2,128)(2,1)} %reshape.431), calls=%async_computation | async-start | bytes 1572864 | tf_op jit(solution)/shard_map/all_to_all | solution.py:67
  86.5 144.2 %all-gather.7.cloned.1.call-start = ((), (), s32[]{:S(2)}) async-start(), calls=%async_computation.3 | async-start | bytes 1081344 | tf_op jit(solution)/shard_map/all_gather | solution.py:102
  165.7 11.6 %copy-start.6 = (f32[1,2048]{1,0:T(1,128)S(1)}, f32[1,2048]{1,0:T(1,128)}, u32[]{:S(2)}) copy-start(f32[1,2048]{1,0:T(1,128)} %param.17) | copy-start | bytes 24580
  176.5 0.6 copy-start.3
  177.1 150.9 %reduce-scatter.4.cloned.1.call-start = ((), (), s32[]{:S(2)}) async-start(), calls=%async_computation.4 | async-start | bytes 14745600
Sparse Core Ops, SparseCore 0:
  9.9 76.9 all-gather.4
  177.2 53.4 all-gather.6
  234.3 93.7 reduce-scatter.3
